TPU v7x, 32 devices: a whole 2x2x4 slice. The times are simulated.
32 devices in a mesh: gx: 2 (over y), gy: 4 (over x, core), gz: 4 (over z).
Axes of the slice: x: 2, y: 2, z: 4, core: 2. Of those that a mesh axis runs over, the one named last changes fastest.
Arguments:
- features: bfloat16 [6, 8, 32, 8, 128], P('gx', 'gy', 'gz'), may hold values from -6 to 6
- positions: float32 [6, 8, 32, 24], P('gx', 'gy', 'gz'), may hold values from 0 to 256, as said below
- grid_anchor: int32 [6, 8, 32, 24], P('gx', 'gy', 'gz'), may hold values from -1 to 254, as said below
- species: int32 [6, 8, 32, 8], P('gx', 'gy', 'gz'), may hold values from 0 to 1
- neighbours: int32 [6, 8, 32, 512], P('gx', 'gy', 'gz'), may hold values from 0 to 12287, as said below
- neighbour_count: int32 [6, 8, 32, 8], P('gx', 'gy', 'gz'), may hold values from 32 to 64
- w_self: bfloat16 [128, 128], replicated, may hold values from -0.5 to 0.5
- w_neighbour: bfloat16 [128, 128], replicated, may hold values from -0.5 to 0.5
- w_radial: bfloat16 [8, 128], replicated, may hold values from -2 to 2
- radial_rates: float32 [8], replicated, may hold values from 0.05 to 2
- w_pair1: bfloat16 [128, 128], replicated, may hold values from -0.5 to 0.5
- w_pair2: bfloat16 [128, 128], replicated, may hold values from -0.5 to 0.5
- w_vector: bfloat16 [128, 128], replicated, may hold values from -0.5 to 0.5
- w_out: bfloat16 [128, 128], replicated, may hold values from -0.5 to 0.5
- w_charge: bfloat16 [128], replicated, may hold values from -0.5 to 0.5
- species_charge: float32 [2], replicated, may hold values from -1 to 1
Outputs:
- features_out: bfloat16 [6, 8, 32, 8, 128], P('gx', 'gy', 'gz')
- site_potential: float32 [6, 8, 32, 8], P('gx', 'gy', 'gz')
Inputs may be any that keep to these rules, and one draw needn't show every extreme that they name: `positions`: component d of slot s of cell (cx, cy, cz) lies in that cell: between c_d * 8 and (c_d + 1) * 8. `grid_anchor`: at the same place as in positions, the whole part of the coordinate minus 1; the coordinate lies between grid_anchor + 1 and grid_anchor + 2. `neighbours`: each entry is the index ((cx * 8 + cy) * 32 + cz) * 8 + s of an atom whose cell differs from the listing atom's cell by at most one along each dimension, periodically; never the listing atom itself.
All inputs are finite; a program needn't handle non-finite values.
Results may differ from a plain program's by a relative error of at most 0.0039.
The roundings to bfloat16 on the way count: a program that leaves them out, or rounds other values in their place, can miss the bound.
Values may be sent and summed in bfloat16 or wider, within the bound.
A program may use at most 64 MiB of HBM per device.

v0:
```python
import functools
import math

import jax
import jax.numpy as jnp
import numpy as np
from jax import lax
from jax.experimental import pallas as pl
from jax.experimental.pallas import tpu as pltpu
from jax.sharding import PartitionSpec as P

NBR = 64
CELL = 8
AXES = ("gx", "gy", "gz")

coulomb_scale = 0.25
smearing = 1.0
highest = lax.Precision.HIGHEST


def padded(block, sides):
    for axis, dim in sides:
        count = lax.axis_size(axis)
        forward = [(i, (i + 1) % count) for i in range(count)]
        backward = [(target, source) for source, target in forward]
        low = lax.ppermute(
            lax.slice_in_dim(block, block.shape[dim] - 1, None, axis=dim), axis, forward
        )
        high = lax.ppermute(lax.slice_in_dim(block, 0, 1, axis=dim), axis, backward)
        block = jnp.concatenate([low, block, high], axis=dim)
    return block


def round_bf16(x):
    return lax.reduce_precision(x, 8, 7)


def three_pieces(x):
    hi = round_bf16(x)
    mid = round_bf16(x - hi)
    lo = round_bf16(x - hi - mid)
    return hi, mid, lo


def cast_pieces(x, count):
    pieces = []
    for _ in range(count):
        piece = x.astype(jnp.bfloat16)
        pieces.append(piece)
        x = x - piece.astype(jnp.float32)
    return pieces


def silu(v):
    half = 0.5 * v
    return half + half * jnp.tanh(half)


def pair_kernel(
    cells,
    lengths,
    code_ref,
    ext_ref,
    own_ref,
    hidden_ref,
    wr_ref,
    rates_ref,
    w1_ref,
    w2_ref,
    wv_ref,
    wo_ref,
    out_ref,
    msg_ref,
    vec_ref,
    w1t_ref,
    w2t_ref,
):
    cells_x, cells_y, cells_z = cells
    f32, bf16 = jnp.float32, jnp.bfloat16
    slots = 8
    pairs = slots * NBR
    w1t_ref[...] = w1_ref[...].astype(f32).T.astype(bf16)
    w2t_ref[...] = w2_ref[...].astype(f32).T.astype(bf16)
    wr_rows = jnp.concatenate([wr_ref[...].astype(f32), jnp.zeros((8, 128), f32)], axis=1)
    zero_half = jnp.zeros((8, 128), f32)
    lane_slot = lax.broadcasted_iota(jnp.int32, (slots, pairs), 1) // NBR
    sel = jnp.where(lane_slot == lax.broadcasted_iota(jnp.int32, (slots, pairs), 0), 1.0, 0.0)
    tail = jnp.concatenate([sel, sel, sel, jnp.zeros((8, pairs), f32)], axis=0).astype(bf16)
    row_d = lax.broadcasted_iota(jnp.int32, (8, 1), 0)
    box = jnp.where(
        row_d == 0,
        float(lengths[0]),
        jnp.where(row_d == 1, float(lengths[1]), float(lengths[2])),
    )
    box_inv = 1.0 / box
    rates = rates_ref[...]

    def one_cell(c, carry):
        cz = c % cells_z
        cxy = c // cells_z
        cy = cxy % cells_y
        cx = cxy // cells_y
        row = pl.multiple_of(cz * 8, 8)
        here = pl.multiple_of(c * 8, 8)
        parts = []
        for dx in range(3):
            for dy in range(3):
                column = (cx + dx) * (cells_y + 2) + cy + dy
                parts.append(ext_ref[column, pl.ds(row, 24), :])
        mine = ext_ref[(cx + 1) * (cells_y + 2) + cy + 1, pl.ds(row + 8, 8), 128:]
        own = own_ref[pl.ds(here, 8), :]
        own_hi, own_mid, own_lo = [p.astype(f32) for p in cast_pieces(own, 3)]
        parts.append(wr_rows)
        parts.append(jnp.concatenate([own_hi, -mine], axis=1))
        parts.append(jnp.concatenate([own_mid, zero_half], axis=1))
        parts.append(jnp.concatenate([own_lo, zero_half], axis=1))
        parts.append(jnp.zeros((8, 256), f32))
        table = jnp.concatenate(parts, axis=0)
        sent_t = table[:, :128].T.astype(bf16)
        place_t = table[:, 128:].T[:32].astype(bf16)
        code = code_ref[c]
        which = code & 255
        live = jnp.where(code < 256, 1.0, 0.0)
        hot = jnp.where(
            lax.broadcasted_iota(jnp.int32, (216, pairs), 0) == which, 1.0, 0.0
        )
        hot_main = hot[:208].astype(bf16)
        hot_last = hot[208:]
        rhs_place = jnp.concatenate(
            [
                hot_main,
                jnp.concatenate([hot_last, jnp.zeros((8, pairs), f32)], axis=0).astype(bf16),
                tail,
            ],
            axis=0,
        )
        found = jnp.dot(place_t, rhs_place, preferred_element_type=f32)
        displace = found[0:8] + found[8:16] + found[16:24]
        displace = displace - box * jnp.floor(displace * box_inv + 0.5)
        scaled = displace * (1.0 / CELL)
        square = jnp.sum(scaled * scaled, axis=0, keepdims=True)
        basis = jnp.exp(-square * rates)
        rhs = jnp.concatenate(
            [hot_main, jnp.concatenate([hot_last, basis], axis=0).astype(bf16), tail], axis=0
        )
        pre = jnp.dot(sent_t, rhs, preferred_element_type=f32)
        latent = silu(pre).astype(bf16)
        second = silu(jnp.dot(w1t_ref[...], latent, preferred_element_type=f32)).astype(bf16)
        third = silu(jnp.dot(w2t_ref[...], second, preferred_element_type=f32)).astype(bf16)
        reach = scaled * live
        pieces = [p.astype(f32) for p in cast_pieces(reach, 3)]
        rows = [sel * live]
        for d in range(3):
            for piece in pieces:
                rows.append(sel * piece[d : d + 1])
        weights = jnp.concatenate(rows, axis=0).astype(bf16)
        sums = lax.dot_general(
            weights, third, (((1,), (1,)), ((), ())), preferred_element_type=f32
        )
        msg_ref[pl.ds(here, 8), :] = sums[0:8] * (1.0 / NBR)
        for d in range(3):
            base = 8 + 24 * d
            vec_ref[d, pl.ds(here, 8), :] = (
                sums[base : base + 8] + sums[base + 8 : base + 16] + sums[base + 16 : base + 24]
            )
        return carry

    lax.fori_loop(0, cells_x * cells_y * cells_z, one_cell, 0)
    wv = wv_ref[...].astype(f32)
    invariant = None
    for d in range(3):
        vector = jnp.dot(
            vec_ref[d], wv, precision=highest, preferred_element_type=f32
        ) * (1.0 / math.sqrt(NBR))
        part = vector * vector
        invariant = part if invariant is None else invariant + part
    update = (msg_ref[...] + invariant).astype(bf16)
    out_ref[...] = (
        hidden_ref[...].astype(f32)
        + jnp.dot(update, wo_ref[...], preferred_element_type=f32)
    ).astype(bf16)


def spline(distance):
    outer = jnp.maximum(2.0 - distance, 0.0)
    inner = jnp.maximum(1.0 - distance, 0.0)
    return (outer * outer * outer - 4.0 * (inner * inner * inner)) * (1.0 / 6.0)


def trig_basis(length):
    r = np.arange(length)
    rows = [np.cos(2 * np.pi * ((k * r) % length) / length) for k in range(length // 2 + 1)]
    rows += [np.sin(2 * np.pi * ((k * r) % length) / length) for k in range(1, length // 2)]
    modes = np.array(list(range(length // 2 + 1)) + list(range(1, length // 2)))
    return np.stack(rows), modes


def axis_terms(modes, length):
    wave = modes * (2.0 * np.pi / length)
    turn = np.exp(2j * np.pi * modes / length)
    modulus = np.abs(1 / 6 + 4 / 6 * turn + 1 / 6 * turn * turn) ** 2
    weight = np.where((modes == 0) | (2 * modes == length), 1.0, 2.0) / length
    return wave * wave, weight / modulus


def charge_kernel(
    sizes,
    lengths,
    window,
    screen,
    planes,
    atoms_ref,
    zrow_ref,
    krow_ref,
    kx_ref,
    by_ref,
    byt_ref,
    bx_ref,
    bxt_ref,
    out_ref,
    plane_ref,
    wave_ref,
):
    devices_x, devices_y, devices_z = sizes
    length_x, length_y, length_z = lengths
    grid_y = length_y // devices_y
    f32, bf16 = jnp.float32, jnp.bfloat16
    lanes = atoms_ref.shape[-1] * devices_z

    def load(gx, gy):
        base = (gx * devices_y + gy) * devices_z
        return jnp.concatenate([atoms_ref[base + i] for i in range(devices_z)], axis=1)

    def stencils(atoms, gy):
        ids_x = lax.broadcasted_iota(jnp.int32, (length_x, lanes), 0).astype(f32)
        off_x = jnp.abs(ids_x - atoms[0:1])
        rows_x = spline(jnp.minimum(off_x, length_x - off_x))
        start = (gy * grid_y - 1).astype(f32)
        ids_y = lax.broadcasted_iota(jnp.int32, (window, lanes), 0).astype(f32)
        rows_y = spline(jnp.abs(ids_y - (atoms[1:2] - start)))
        return rows_x, rows_y

    zrow = zrow_ref[...]

    def spread(gx, gy):
        atoms = load(gx, gy)
        rows_x, rows_y = stencils(atoms, gy)
        place_z = atoms[2:3]
        whole = jnp.floor(place_z)
        f = place_z - whole
        sq = f * f
        cube = sq * f
        rem = 1.0 - f
        taps = [
            rem * rem * rem * (1.0 / 6.0),
            (3.0 * cube - 6.0 * sq + 4.0) * (1.0 / 6.0),
            (-3.0 * cube + 3.0 * sq + 3.0 * f + 1.0) * (1.0 / 6.0),
            cube * (1.0 / 6.0),
        ]
        turns = zrow[:, 0:1] * (whole - 1.0)
        turns = turns - length_z * jnp.floor(turns * (1.0 / length_z))
        angle = (turns - 0.5 * length_z) * (2.0 * math.pi / length_z)
        cos_a = -jnp.cos(angle)
        sin_a = -jnp.sin(angle)
        shift_c = zrow[:, 1:2]
        shift_s = zrow[:, 2:3]
        base_c = cos_a * shift_c + sin_a * shift_s
        base_s = sin_a * shift_c - cos_a * shift_s
        even = taps[0]
        odd = 0.0
        for t in range(1, 4):
            even = even + taps[t] * zrow[:, 2 + t : 3 + t]
            odd = odd + taps[t] * zrow[:, 5 + t : 6 + t]
        wave = base_c * even - base_s * odd
        wave_ref[gx * devices_y + gy] = wave
        scaled = wave * atoms[3:4]
        left = jnp.concatenate([rows_y * scaled[j : j + 1] for j in range(planes)], axis=0)
        left_hi = left.astype(bf16)
        left_lo = (left - left_hi.astype(f32)).astype(bf16)
        x_hi = rows_x.astype(bf16)
        x_lo = (rows_x - x_hi.astype(f32)).astype(bf16)
        res = lax.dot_general(
            jnp.concatenate([left_hi, left_lo], axis=0),
            jnp.concatenate([x_hi, x_lo], axis=0),
            (((1,), (1,)), ((), ())),
            preferred_element_type=f32,
        )
        half = planes * window
        res = res[:half] + res[half:]
        return res[:, :length_x] + res[:, length_x:]

    for gy in range(devices_y):
        gy_id = jnp.int32(gy)
        total = lax.fori_loop(
            0,
            devices_x,
            lambda gx, acc: acc + spread(gx, gy_id),
            jnp.zeros((planes * window, length_x), f32),
        )
        for j in range(planes):
            plane_ref[j, gy * window : (gy + 1) * window, :] = total[
                j * window : (j + 1) * window
            ]

    def hdot(a, b):
        return jnp.dot(a, b, precision=highest, preferred_element_type=f32)

    along_y = jnp.concatenate([hdot(by_ref[...], plane_ref[j]) for j in range(planes)], axis=0)
    spectrum = hdot(along_y, bxt_ref[...])
    krow = krow_ref[...]
    q = krow[:, 0:1] + kx_ref[0:1, :]
    scale = krow[:, 1:2] * kx_ref[1:2, :]
    green = (coulomb_scale * 4.0 * math.pi) * jnp.exp(-0.5 * smearing * smearing * q)
    green = green * scale / (q + 1.0 / (screen * screen))
    green = jnp.where(q == 0.0, 0.0, green)
    back = hdot(spectrum * green, bx_ref[...])
    for j in range(planes):
        plane_ref[j] = hdot(byt_ref[...], back[j * length_y : (j + 1) * length_y])

    for gy in range(devices_y):
        gy_id = jnp.int32(gy)
        field = jnp.concatenate(
            [plane_ref[j, gy * window : (gy + 1) * window, :] for j in range(planes)], axis=0
        )
        f_hi, f_mid = [p.astype(f32) for p in cast_pieces(field, 2)]
        field3 = jnp.concatenate([f_hi, f_mid, f_hi], axis=1).astype(bf16)

        def sample(gx, carry):
            atoms = load(gx, gy_id)
            rows_x, rows_y = stencils(atoms, gy_id)
            x_hi = rows_x.astype(bf16)
            x_lo = (rows_x - x_hi.astype(f32)).astype(bf16)
            values = jnp.dot(
                field3,
                jnp.concatenate([x_hi, x_hi, x_lo], axis=0),
                preferred_element_type=f32,
            )
            wave = wave_ref[gx * devices_y + gy_id]
            mixed = values[0:window] * wave[0:1]
            for j in range(1, planes):
                mixed = mixed + values[j * window : (j + 1) * window] * wave[j : j + 1]
            out_ref[gx * devices_y + gy_id] = jnp.sum(mixed * rows_y, axis=0, keepdims=True)
            return carry

        lax.fori_loop(0, devices_x, sample, 0)


def shards(
    features,
    positions,
    grid_anchor,
    species,
    neighbours,
    neighbour_count,
    w_self,
    w_neighbour,
    w_radial,
    radial_rates,
    w_pair1,
    w_pair2,
    w_vector,
    w_out,
    w_charge,
    species_charge,
):
    f32, bf16 = jnp.float32, jnp.bfloat16
    cells_x, cells_y, cells_z, slot_count, channels = features.shape
    cell_count = cells_x * cells_y * cells_z
    atom_count = cell_count * slot_count
    sizes = tuple(lax.axis_size(a) for a in AXES)
    devices = sizes[0] * sizes[1] * sizes[2]
    totals = (cells_x * sizes[0], cells_y * sizes[1], cells_z * sizes[2])
    lengths = tuple(t * CELL for t in totals)
    length_x, length_y, length_z = lengths
    screen = 2 * cells_y * CELL

    hidden = features.reshape(atom_count, channels)
    own = jnp.dot(hidden, w_self, preferred_element_type=f32)
    sent = jnp.dot(hidden, w_neighbour, preferred_element_type=f32).astype(bf16)
    species_rows = species.reshape(atom_count)
    kind_ids = jnp.arange(species_charge.shape[0], dtype=jnp.int32)
    base_charge = jnp.sum(
        jnp.where(species_rows[:, None] == kind_ids[None, :], species_charge[None, :], 0.0), axis=1
    )
    charge = base_charge + jnp.dot(hidden, w_charge, preferred_element_type=f32)
    place = positions.reshape(cell_count, 3, slot_count)
    place_cols = jnp.moveaxis(place, 1, 0).reshape(3, atom_count)
    atoms = jnp.concatenate([place_cols, charge[None]], axis=0)
    atoms = lax.all_gather(atoms, AXES)

    hi, mid, lo = three_pieces(jnp.moveaxis(place, 1, 2).reshape(atom_count, 3))
    gap = jnp.zeros((atom_count, 5), f32)
    place_rows = jnp.concatenate(
        [hi, gap, mid, gap, lo, gap, jnp.zeros((atom_count, channels - 24), f32)], axis=1
    ).astype(bf16)
    rows = jnp.concatenate([sent, place_rows], axis=1)
    rows = rows.reshape(cells_x, cells_y, cells_z, slot_count, 2 * channels)
    ext = padded(rows, (("gx", 0), ("gy", 1), ("gz", 2)))
    ext = ext.astype(f32).reshape(
        (cells_x + 2) * (cells_y + 2), (cells_z + 2) * slot_count, 2 * channels
    )

    listed = neighbours.reshape(cells_x, cells_y, cells_z, slot_count * NBR)
    slot_ids = listed % slot_count
    cell_ids = listed // slot_count
    steps = []
    for axis, ids in enumerate(
        (cell_ids // (totals[2] * totals[1]), cell_ids // totals[2] % totals[1], cell_ids % totals[2])
    ):
        local = lax.broadcasted_iota(jnp.int32, listed.shape, axis)
        first = lax.axis_index(AXES[axis]) * (cells_x, cells_y, cells_z)[axis]
        steps.append((ids - first - local + 1 + totals[axis]) % totals[axis])
    code = ((steps[0] * 3 + steps[1]) * 3 + steps[2]) * slot_count + slot_ids
    counts = neighbour_count.reshape(cell_count, slot_count, 1)
    dead = jnp.arange(NBR, dtype=jnp.int32)[None, None, :] >= counts
    code = code.reshape(cell_count, slot_count, NBR) + jnp.where(dead, 256, 0)
    code = code.reshape(cell_count, 1, slot_count * NBR)

    vmem = pl.BlockSpec(memory_space=pltpu.VMEM)
    updated = pl.pallas_call(
        functools.partial(pair_kernel, (cells_x, cells_y, cells_z), lengths),
        out_shape=jax.ShapeDtypeStruct((atom_count, channels), bf16),
        in_specs=[vmem] * 10,
        out_specs=vmem,
        scratch_shapes=[
            pltpu.VMEM((atom_count, channels), f32),
            pltpu.VMEM((3, atom_count, channels), f32),
            pltpu.VMEM((channels, channels), bf16),
            pltpu.VMEM((channels, channels), bf16),
        ],
        name="pair_layer",
        cost_estimate=pl.CostEstimate(
            flops=2 * atom_count * NBR * channels * 512,
            bytes_accessed=4 * 1024 * 1024,
            transcendentals=3 * atom_count * NBR * channels,
        ),
    )(
        code,
        ext,
        own,
        hidden,
        w_radial,
        radial_rates.reshape(-1, 1),
        w_pair1,
        w_pair2,
        w_vector,
        w_out,
    )

    share = length_z // 2 // devices
    planes = 2 * share
    window = -(-(cells_y * CELL + 4) // 8) * 8
    all_modes = np.arange(length_z // 2)
    table_k = np.stack([all_modes, all_modes], axis=1)
    phase_c = np.stack([np.ones_like(all_modes), np.zeros_like(all_modes)], axis=1)
    table_k[0, 1] = length_z // 2
    phase_c[0, 1] = 1
    table_k = table_k.reshape(devices, planes)
    phase_c = phase_c.reshape(devices, planes).astype(np.float64)
    taps = [2 * np.pi * ((table_k * t) % length_z) / length_z for t in range(1, 4)]
    zrow = np.stack(
        [table_k, phase_c, 1.0 - phase_c]
        + [np.cos(a) for a in taps]
        + [np.sin(a) for a in taps],
        axis=2,
    ).astype(np.float32)
    basis_x, modes_x = trig_basis(length_x)
    basis_y, modes_y = trig_basis(length_y)
    qx, sx = axis_terms(modes_x, length_x)
    qy, sy = axis_terms(modes_y, length_y)
    qz, sz = axis_terms(table_k, length_z)
    krow = np.stack(
        [qz[:, :, None] + qy[None, None, :], sz[:, :, None] * sy[None, None, :]], axis=-1
    )
    krow = krow.reshape(devices, planes * length_y, 2).astype(np.float32)
    kx = np.stack([qx, sx]).astype(np.float32)
    grid_y = cells_y * CELL
    columns = np.concatenate(
        [(np.arange(window) + g * grid_y - 1) % length_y for g in range(sizes[1])]
    )
    by = basis_y[:, columns].astype(np.float32)
    bx = basis_x.astype(np.float32)
    me = lax.axis_index(AXES)
    partial = pl.pallas_call(
        functools.partial(charge_kernel, sizes, lengths, window, screen, planes),
        out_shape=jax.ShapeDtypeStruct((sizes[0] * sizes[1], 1, sizes[2] * atom_count), f32),
        in_specs=[vmem] * 8,
        out_specs=vmem,
        scratch_shapes=[
            pltpu.VMEM((planes, sizes[1] * window, length_x), f32),
            pltpu.VMEM((sizes[0] * sizes[1], planes, sizes[2] * atom_count), f32),
        ],
        name="charge_solve",
        cost_estimate=pl.CostEstimate(
            flops=10**10, bytes_accessed=2 * 1024 * 1024, transcendentals=10**6
        ),
    )(
        atoms,
        lax.dynamic_index_in_dim(jnp.asarray(zrow), me, 0, False),
        lax.dynamic_index_in_dim(jnp.asarray(krow), me, 0, False),
        jnp.asarray(kx),
        jnp.asarray(by),
        jnp.asarray(np.ascontiguousarray(by.T)),
        jnp.asarray(bx),
        jnp.asarray(np.ascontiguousarray(bx.T)),
    )
    site_potential = lax.psum_scatter(
        partial.reshape(devices, atom_count), AXES, scatter_dimension=0, tiled=False
    )
    return (
        updated.reshape(features.shape),
        site_potential.reshape(cells_x, cells_y, cells_z, slot_count),
    )


def solution(mesh):
    return jax.shard_map(
        shards,
        mesh=mesh,
        in_specs=(
            P("gx", "gy", "gz", None, None),
            P("gx", "gy", "gz", None),
            P("gx", "gy", "gz", None),
            P("gx", "gy", "gz", None),
            P("gx", "gy", "gz", None),
            P("gx", "gy", "gz", None),
            P(),
            P(),
            P(),
            P(),
            P(),
            P(),
            P(),
            P(),
            P(),
            P(),
        ),
        out_specs=(P("gx", "gy", "gz", None, None), P("gx", "gy", "gz", None)),
        check_vma=False,
    )
```

profile of v0, /device:TPU:0, one launch (start us, length us, event | category | flops | bytes accessed | tf_op | source)
XLA Modules:
  0.0 201.9 jit_solution(3467196935086238243)
XLA Ops:
  0.6 0.8 copy.44
  1.8 1.1 convolution_convert_fusion
  3.3 3.1 %collective-permute-start = (bf16[1,2,8,8,256]{4,3,2,1,0:T(8,128)(2,1)S(1)}, bf16[1,2,8,8,256]{4,3,2,1,0:T(8,128)(2,1)S(1)}, u32[]{:S(2)}, u32[]{:S(2)}) collective-permute-start(bf16[1,2,8,8,256]{4,3,2,1,0:T(8,128)(2,1)S(1)} %bitcast.43), channel_id=1, source_target_pairs={{0,16},{16,0},{1,17},{17,1},{2,18},{18,2},{3,19},{19,3},{4,20},{20... | collective-permute-start | bytes 196616 | tf_op jit(solution)/shard_map/ppermute | solution.py:26
  6.5 1.7 dynamic-slice_bitcast_fusion.krow_ref
  8.2 1.3 dynamic-slice_bitcast_fusion.1.zrow_ref
  9.5 1.0 convolution_reduce_fusion
  10.5 0.8 eq.22
  11.3 0.7 fusion.25
  12.3 74.5 %all-gather.1.atoms_ref = f32[32,4,384]{2,1,0:T(4,128)} all-gather(f32[1,4,384]{2,1,0:T(4,128)S(1)} %maximum_bitcast_fusion), channel_id=2, replica_groups=mesh['gx'=2,'gy'=4,'gz'=4] {'gx','gy','gz'}, dimensions={0}, use_global_device_ids=true | all-gather | bytes 202752 | tf_op jit(solution)/shard_map/all_gather | solution.py:389
  86.9 16.0 %charge_solve.1 = f32[8,1,1536]{2,1,0:T(1,128)} custom-call(f32[32,4,384]{2,1,0:T(4,128)} %all-gather.1.atoms_ref, f32[8,9]{1,0:T(8,128)} %dynamic-slice_bitcast_fusion.1.zrow_ref, f32[512,2]{1,0:T(8,128)} %dynamic-slice_bitcast_fusion.krow_ref, f32[2,48]{1,0:T(2,128)} %constant.143.clone.kx_ref, f32[64,96]{1,0:T(8,128)} %constant.144.clone.by_ref, ...), custom_call_target="tpu_custom_call" | custom-call | flops 10000000000 | bytes 2097152 | tf_op jit(solution)/shard_map/charge_solve/pallas_call | solution.py:484
  102.9 0.4 fusion.10
  103.7 0.2 ge.33
  104.1 1.7 collective-permute-start.3
  105.8 0.8 fusion.29.own_ref
  106.6 2.2 %collective-permute-done.2 = bf16[5,1,8,8,256]{4,3,2,1,0:T(8,128)(2,1)S(1)} collective-permute-done((bf16[5,1,8,8,256]{4,3,2,1,0:T(8,128)(2,1)S(1)}, bf16[5,1,8,8,256]{4,3,2,1,0:T(8,128)(2,1)S(1)}, u32[]{:S(2)}, u32[]{:S(2)}) %collective-permute-start.2) | collective-permute-done | bytes 163872 | tf_op jit(solution)/shard_map/ppermute | solution.py:26
  108.9 3.8 %collective-permute-start.5 = (bf16[5,4,1,8,256]{4,3,2,1,0:T(8,128)(2,1)S(1)}, bf16[5,4,1,8,256]{4,3,2,1,0:T(8,128)(2,1)S(1)}, u32[]{:S(2)}, u32[]{:S(2)}) collective-permute-start(bf16[5,4,1,8,256]{4,3,2,1,0:T(8,128)(2,1)S(1)} %get-tuple-element.3), channel_id=1, source_target_pairs={{1,0},{2,1},{3,2},{0,3},{5,4},{6,5},{7,6},{4,7},{9,8},{10,9},{11,1... | collective-permute-start | bytes 245768 | tf_op jit(solution)/shard_map/ppermute | solution.py:29
  112.7 0.8 fusion.20.code_ref
  113.5 0.7 copy.49.rates_ref
  114.1 0.9 reduce.1
  115.1 37.3 %all-reduce = f32[32,384]{1,0:T(8,128)S(1)} all-reduce(f32[32,384]{1,0:T(8,128)S(1)} %reshape.97), channel_id=3, replica_groups=mesh['gx'=2,'gy'=4,'gz'=4] {'gx','gy','gz'}, use_global_device_ids=true, to_apply=%region_1.2.clone | all-reduce | flops 12288 | bytes 98304
  152.4 0.7 reshape_reduce_scatter.3
  153.1 0.2 pad_maximum_fusion
  153.2 1.4 convert.21.ext_ref
  154.6 47.3 %pair_layer.1 = bf16[384,128]{1,0:T(8,128)(2,1)} custom-call(s32[48,1,512]{2,1,0:T(1,128)} %fusion.20.code_ref, f32[20,80,256]{2,1,0:T(8,128)} %convert.21.ext_ref, f32[384,128]{1,0:T(8,128)} %fusion.29.own_ref, bf16[384,128]{1,0:T(8,128)(2,1)} %bitcast.39, bf16[8,128]{1,0:T(8,128)(2,1)} %wr_ref.1, f32[8,1]{1,0:T(8,128)} %copy.49.rates_ref, ...), custom_call_target="tpu_custom_call" | custom-call | flops 3221225472 | bytes 4194304 | tf_op jit(solution)/shard_map/pair_layer/pallas_call | solution.py:420
  (45 shorter events, 1.7 us)
Async XLA Ops:
  0.6 1.2 copy-start
  3.3 100.7 %collective-permute-start = (bf16[1,2,8,8,256]{4,3,2,1,0:T(8,128)(2,1)S(1)}, bf16[1,2,8,8,256]{4,3,2,1,0:T(8,128)(2,1)S(1)}, u32[]{:S(2)}, u32[]{:S(2)}) collective-permute-start(bf16[1,2,8,8,256]{4,3,2,1,0:T(8,128)(2,1)S(1)} %bitcast.43), channel_id=1, source_target_pairs={{0,16},{16,0},{1,17},{17,1},{2,18},{18,2},{3,19},{19,3},{4,20},{20... | collective-permute-start | bytes 196616 | tf_op jit(solution)/shard_map/ppermute | solution.py:26
  6.4 97.5 %collective-permute-start.1 = (bf16[1,2,8,8,256]{4,3,2,1,0:T(8,128)(2,1)S(1)}, bf16[1,2,8,8,256]{4,3,2,1,0:T(8,128)(2,1)S(1)}, u32[]{:S(2)}, u32[]{:S(2)}) collective-permute-start(bf16[1,2,8,8,256]{4,3,2,1,0:T(8,128)(2,1)S(1)} %bitcast.44), channel_id=1, source_target_pairs={{16,0},{0,16},{17,1},{1,17},{18,2},{2,18},{19,3},{3,19},{20,4},{4,... | collective-permute-start | bytes 196616 | tf_op jit(solution)/shard_map/ppermute | solution.py:29
  86.9 16.0 %copy-start.2 = (s32[3,2,8,512]{3,2,1,0:T(8,128)S(1)}, s32[3,2,8,512]{3,2,1,0:T(8,128)}, u32[]{:S(2)}) copy-start(s32[3,2,8,512]{3,2,1,0:T(8,128)} %param.26) | copy-start | bytes 294916
  86.9 16.7 %copy-start.4 = (s32[3,2,8,8]{3,2,1,0:T(8,128)S(1)}, s32[3,2,8,8]{3,2,1,0:T(8,128)}, u32[]{:S(2)}) copy-start(s32[3,2,8,8]{3,2,1,0:T(8,128)} %param.27) | copy-start | bytes 4612
  86.9 18.9 %copy-start.1 = (bf16[3,2,8,8,128]{4,3,2,1,0:T(8,128)(2,1)S(1)}, bf16[3,2,8,8,128]{4,3,2,1,0:T(8,128)(2,1)}, u32[]{:S(2)}) copy-start(bf16[3,2,8,8,128]{4,3,2,1,0:T(8,128)(2,1)} %param.23) | copy-start | bytes 294916
  86.9 18.9 %copy-start.3 = (bf16[128,128]{1,0:T(8,128)(2,1)S(1)}, bf16[128,128]{1,0:T(8,128)(2,1)}, u32[]{:S(2)}) copy-start(bf16[128,128]{1,0:T(8,128)(2,1)} %param.28) | copy-start | bytes 98308
  86.9 26.6 %copy-start.5 = (f32[8]{0:T(128)S(1)}, f32[8]{0:T(128)}, u32[]{:S(2)}) copy-start(f32[8]{0:T(128)} %param.31) | copy-start | bytes 100
  104.0 4.8 %collective-permute-start.2 = (bf16[5,1,8,8,256]{4,3,2,1,0:T(8,128)(2,1)S(1)}, bf16[5,1,8,8,256]{4,3,2,1,0:T(8,128)(2,1)S(1)}, u32[]{:S(2)}, u32[]{:S(2)}) collective-permute-start(bf16[5,1,8,8,256]{4,3,2,1,0:T(8,128)(2,1)S(1)} %get-tuple-element.4), channel_id=1, source_target_pairs={{0,4},{4,8},{8,12},{12,0},{1,5},{5,9},{9,13},{13,1},{2,6},{6,10},{... | collective-permute-start | bytes 491528 | tf_op jit(solution)/shard_map/ppermute | solution.py:26
  104.1 4.7 %collective-permute-start.3 = (bf16[5,1,8,8,256]{4,3,2,1,0:T(8,128)(2,1)S(1)}, bf16[5,1,8,8,256]{4,3,2,1,0:T(8,128)(2,1)S(1)}, u32[]{:S(2)}, u32[]{:S(2)}) collective-permute-start(bf16[5,1,8,8,256]{4,3,2,1,0:T(8,128)(2,1)S(1)} %get-tuple-element.5), channel_id=1, source_target_pairs={{4,0},{8,4},{12,8},{0,12},{5,1},{9,5},{13,9},{1,13},{6,2},{10,6},{... | collective-permute-start | bytes 491528 | tf_op jit(solution)/shard_map/ppermute | solution.py:29
  108.8 44.3 %collective-permute-start.4 = (bf16[5,4,1,8,256]{4,3,2,1,0:T(8,128)(2,1)S(1)}, bf16[5,4,1,8,256]{4,3,2,1,0:T(8,128)(2,1)S(1)}, u32[]{:S(2)}, u32[]{:S(2)}) collective-permute-start(bf16[5,4,1,8,256]{4,3,2,1,0:T(8,128)(2,1)S(1)} %get-tuple-element.2), channel_id=1, source_target_pairs={{0,1},{1,2},{2,3},{3,0},{4,5},{5,6},{6,7},{7,4},{8,9},{9,10},{10,1... | collective-permute-start | bytes 245768 | tf_op jit(solution)/shard_map/ppermute | solution.py:26
  108.9 44.2 %collective-permute-start.5 = (bf16[5,4,1,8,256]{4,3,2,1,0:T(8,128)(2,1)S(1)}, bf16[5,4,1,8,256]{4,3,2,1,0:T(8,128)(2,1)S(1)}, u32[]{:S(2)}, u32[]{:S(2)}) collective-permute-start(bf16[5,4,1,8,256]{4,3,2,1,0:T(8,128)(2,1)S(1)} %get-tuple-element.3), channel_id=1, source_target_pairs={{1,0},{2,1},{3,2},{0,3},{5,4},{6,5},{7,6},{4,7},{9,8},{10,9},{11,1... | collective-permute-start | bytes 245768 | tf_op jit(solution)/shard_map/ppermute | solution.py:29
where the time goes:
time: 203 us; the launch traced here: 202 us
  blocking collectives  112 us (55%)
  Pallas kernels  63.3 us (31%)
  starting transfers between devices  8.8 us (4%)
  local copies, waits for them, and re-layouts  7.55 us (4%)
  other arithmetic  4.45 us (2%)
  matrix products  3 us (1%)
  waiting for transfers between devices  2.16 us (1%)
    all_gather x1, blocking collectives, shards(): atoms = lax.all_gather(atoms, AXES)  74.5 us
    pallas_call x1, Pallas kernels, shards(): pl.pallas_call(functools.partial(pair_kernel, (cells_x, cells_y, cells_z)...  47.3 us
    unnamed x1, blocking collectives  37.3 us
    pallas_call x1, Pallas kernels, shards(): pl.pallas_call(functools.partial(charge_kernel, sizes, lengths, window, s...  16 us
    ppermute x3, starting transfers between devices, padded(): high = lax.ppermute(lax.slice_in_dim(block, 0, 1, axis=dim), axis, backward)  5.62 us
  transfers between devices with their start and end apart: 6, of which 1 were waited for; matrix products, arithmetic and copies ran while one was open for 5% of the time, Pallas kernels for 8%

commit v1 on v0

--- a/solution.py
+++ b/solution.py
@@ -16,19 +16,6 @@
 coulomb_scale = 0.25
 smearing = 1.0
 highest = lax.Precision.HIGHEST
-
-
-def padded(block, sides):
-    for axis, dim in sides:
-        count = lax.axis_size(axis)
-        forward = [(i, (i + 1) % count) for i in range(count)]
-        backward = [(target, source) for source, target in forward]
-        low = lax.ppermute(
-            lax.slice_in_dim(block, block.shape[dim] - 1, None, axis=dim), axis, forward
-        )
-        high = lax.ppermute(lax.slice_in_dim(block, 0, 1, axis=dim), axis, backward)
-        block = jnp.concatenate([low, block, high], axis=dim)
-    return block
 
 
 def round_bf16(x):
@@ -240,7 +227,7 @@
         rows_y = spline(jnp.abs(ids_y - (atoms[1:2] - start)))
         return rows_x, rows_y
 
-    zrow = zrow_ref[...]
+    zrow = zrow_ref[my_index(sizes)]
 
     def spread(gx, gy):
         atoms = load(gx, gy)
@@ -289,60 +276,180 @@
         res = res[:half] + res[half:]
         return res[:, :length_x] + res[:, length_x:]
 
-    for gy in range(devices_y):
-        gy_id = jnp.int32(gy)
-        total = lax.fori_loop(
-            0,
-            devices_x,
-            lambda gx, acc: acc + spread(gx, gy_id),
-            jnp.zeros((planes * window, length_x), f32),
-        )
+    plane_ref[...] = jnp.zeros(plane_ref.shape, f32)
+
+    def spread_group(g, carry):
+        gy = g % devices_y
+        total = spread(g // devices_y, gy)
+        rows = pl.ds(pl.multiple_of(gy * window, 8), window)
         for j in range(planes):
-            plane_ref[j, gy * window : (gy + 1) * window, :] = total[
-                j * window : (j + 1) * window
-            ]
+            plane_ref[j, rows, :] += total[j * window : (j + 1) * window]
+        return carry
+
+    lax.fori_loop(0, devices_x * devices_y, spread_group, 0)
 
     def hdot(a, b):
         return jnp.dot(a, b, precision=highest, preferred_element_type=f32)
 
     along_y = jnp.concatenate([hdot(by_ref[...], plane_ref[j]) for j in range(planes)], axis=0)
     spectrum = hdot(along_y, bxt_ref[...])
-    krow = krow_ref[...]
-    q = krow[:, 0:1] + kx_ref[0:1, :]
-    scale = krow[:, 1:2] * kx_ref[1:2, :]
-    green = (coulomb_scale * 4.0 * math.pi) * jnp.exp(-0.5 * smearing * smearing * q)
-    green = green * scale / (q + 1.0 / (screen * screen))
-    green = jnp.where(q == 0.0, 0.0, green)
-    back = hdot(spectrum * green, bx_ref[...])
+    kcol = krow_ref[...]
+    filtered = []
+    for j in range(planes):
+        q = kcol[:, 0:1] + zrow[j : j + 1, 9:10] + kx_ref[0:1, :]
+        scale = kcol[:, 1:2] * zrow[j : j + 1, 10:11] * kx_ref[1:2, :]
+        green = (coulomb_scale * 4.0 * math.pi) * jnp.exp(-0.5 * smearing * smearing * q)
+        green = green * scale / (q + 1.0 / (screen * screen))
+        green = jnp.where(q == 0.0, 0.0, green)
+        filtered.append(spectrum[j * length_y : (j + 1) * length_y] * green)
+    back = hdot(jnp.concatenate(filtered, axis=0), bx_ref[...])
     for j in range(planes):
         plane_ref[j] = hdot(byt_ref[...], back[j * length_y : (j + 1) * length_y])
 
-    for gy in range(devices_y):
-        gy_id = jnp.int32(gy)
-        field = jnp.concatenate(
-            [plane_ref[j, gy * window : (gy + 1) * window, :] for j in range(planes)], axis=0
-        )
+    def sample_group(g, carry):
+        gy = g % devices_y
+        rows = pl.ds(pl.multiple_of(gy * window, 8), window)
+        field = jnp.concatenate([plane_ref[j, rows, :] for j in range(planes)], axis=0)
         f_hi, f_mid = [p.astype(f32) for p in cast_pieces(field, 2)]
         field3 = jnp.concatenate([f_hi, f_mid, f_hi], axis=1).astype(bf16)
-
-        def sample(gx, carry):
-            atoms = load(gx, gy_id)
-            rows_x, rows_y = stencils(atoms, gy_id)
-            x_hi = rows_x.astype(bf16)
-            x_lo = (rows_x - x_hi.astype(f32)).astype(bf16)
-            values = jnp.dot(
-                field3,
-                jnp.concatenate([x_hi, x_hi, x_lo], axis=0),
-                preferred_element_type=f32,
-            )
-            wave = wave_ref[gx * devices_y + gy_id]
-            mixed = values[0:window] * wave[0:1]
-            for j in range(1, planes):
-                mixed = mixed + values[j * window : (j + 1) * window] * wave[j : j + 1]
-            out_ref[gx * devices_y + gy_id] = jnp.sum(mixed * rows_y, axis=0, keepdims=True)
-            return carry
-
-        lax.fori_loop(0, devices_x, sample, 0)
+        atoms = load(g // devices_y, gy)
+        rows_x, rows_y = stencils(atoms, gy)
+        x_hi = rows_x.astype(bf16)
+        x_lo = (rows_x - x_hi.astype(f32)).astype(bf16)
+        values = jnp.dot(
+            field3, jnp.concatenate([x_hi, x_hi, x_lo], axis=0), preferred_element_type=f32
+        )
+        wave = wave_ref[g]
+        mixed = values[0:window] * wave[0:1]
+        for j in range(1, planes):
+            mixed = mixed + values[j * window : (j + 1) * window] * wave[j : j + 1]
+        line = jnp.sum(mixed * rows_y, axis=0, keepdims=True)
+        count = atoms_ref.shape[-1]
+        for i in range(devices_z):
+            out_ref[g * devices_z + i] = line[:, i * count : (i + 1) * count]
+        return carry
+
+    lax.fori_loop(0, devices_x * devices_y, sample_group, 0)
+
+
+def coords_of(index, sizes):
+    return (
+        index // (sizes[1] * sizes[2]),
+        (index // sizes[2]) % sizes[1],
+        index % sizes[2],
+    )
+
+
+def my_index(sizes):
+    gx, gy, gz = (lax.axis_index(a) for a in AXES)
+    return (gx * sizes[1] + gy) * sizes[2] + gz
+
+
+def gather_kernel(
+    sizes, cells, atoms_ref, rows_ref, all_ref, ext_ref, asend, arecv, hsend, hrecv, local_sem
+):
+    devices = sizes[0] * sizes[1] * sizes[2]
+    here = tuple(lax.axis_index(a) for a in AXES)
+    me = my_index(sizes)
+    copies = []
+    for shift in range(27):
+        step = (shift // 9 - 1, shift // 3 % 3 - 1, shift % 3 - 1)
+        if step == (0, 0, 0):
+            continue
+        source, target, peer = [], [], []
+        for axis in range(3):
+            size = cells[axis]
+            if step[axis] == 0:
+                source.append(pl.ds(0, size))
+                target.append(pl.ds(1, size))
+                peer.append(here[axis])
+            elif step[axis] > 0:
+                source.append(pl.ds(size - 1, 1))
+                target.append(pl.ds(0, 1))
+                peer.append(lax.rem(here[axis] + 1, sizes[axis]))
+            else:
+                source.append(pl.ds(0, 1))
+                target.append(pl.ds(size + 1, 1))
+                peer.append(lax.rem(here[axis] + sizes[axis] - 1, sizes[axis]))
+        copy = pltpu.make_async_remote_copy(
+            src_ref=rows_ref.at[tuple(source)],
+            dst_ref=ext_ref.at[tuple(target)],
+            send_sem=hsend.at[shift],
+            recv_sem=hrecv.at[shift],
+            device_id=tuple(peer),
+            device_id_type=pl.DeviceIdType.MESH,
+        )
+        copies.append(copy)
+
+    def atom_copy(o):
+        peer = lax.rem(me + o, devices)
+        return pltpu.make_async_remote_copy(
+            src_ref=atoms_ref,
+            dst_ref=all_ref.at[me],
+            send_sem=asend.at[o],
+            recv_sem=arecv.at[o],
+            device_id=coords_of(peer, sizes),
+            device_id_type=pl.DeviceIdType.MESH,
+        )
+
+    def start(o, carry):
+        atom_copy(o).start()
+        return carry
+
+    lax.fori_loop(1, devices, start, 0)
+    for copy in copies:
+        copy.start()
+    inner = tuple(pl.ds(1, size) for size in cells)
+    local = pltpu.make_async_copy(rows_ref, ext_ref.at[inner], local_sem.at[0])
+    local.start()
+    local_atoms = pltpu.make_async_copy(atoms_ref, all_ref.at[me], local_sem.at[1])
+    local_atoms.start()
+    local.wait()
+    local_atoms.wait()
+
+    def finish(o, carry):
+        origin = lax.rem(me + devices - o, devices)
+        pltpu.make_async_remote_copy(
+            src_ref=atoms_ref,
+            dst_ref=all_ref.at[origin],
+            send_sem=asend.at[o],
+            recv_sem=arecv.at[o],
+            device_id=coords_of(origin, sizes),
+            device_id_type=pl.DeviceIdType.MESH,
+        ).wait()
+        return carry
+
+    lax.fori_loop(1, devices, finish, 0)
+    for copy in copies:
+        copy.wait()
+
+
+def scatter_kernel(sizes, part_ref, out_ref, held_ref, send, recv):
+    devices = sizes[0] * sizes[1] * sizes[2]
+    me = my_index(sizes)
+
+    def copy_to(o):
+        peer = lax.rem(me + o, devices)
+        return pltpu.make_async_remote_copy(
+            src_ref=part_ref.at[peer],
+            dst_ref=held_ref.at[o],
+            send_sem=send.at[o],
+            recv_sem=recv.at[o],
+            device_id=coords_of(peer, sizes),
+            device_id_type=pl.DeviceIdType.MESH,
+        )
+
+    def start(o, carry):
+        copy_to(o).start()
+        return carry
+
+    lax.fori_loop(1, devices, start, 0)
+
+    def finish(o, total):
+        copy_to(o).wait()
+        return total + held_ref[o]
+
+    out_ref[...] = lax.fori_loop(1, devices, finish, part_ref[me])
 
 
 def shards(
@@ -386,7 +493,6 @@
     place = positions.reshape(cell_count, 3, slot_count)
     place_cols = jnp.moveaxis(place, 1, 0).reshape(3, atom_count)
     atoms = jnp.concatenate([place_cols, charge[None]], axis=0)
-    atoms = lax.all_gather(atoms, AXES)
 
     hi, mid, lo = three_pieces(jnp.moveaxis(place, 1, 2).reshape(atom_count, 3))
     gap = jnp.zeros((atom_count, 5), f32)
@@ -395,7 +501,23 @@
     ).astype(bf16)
     rows = jnp.concatenate([sent, place_rows], axis=1)
     rows = rows.reshape(cells_x, cells_y, cells_z, slot_count, 2 * channels)
-    ext = padded(rows, (("gx", 0), ("gy", 1), ("gz", 2)))
+    cells = (cells_x, cells_y, cells_z)
+    vmem = pl.BlockSpec(memory_space=pltpu.VMEM)
+    dma = pltpu.SemaphoreType.DMA
+    atoms, ext = pl.pallas_call(
+        functools.partial(gather_kernel, sizes, cells),
+        out_shape=(
+            jax.ShapeDtypeStruct((devices,) + atoms.shape, f32),
+            jax.ShapeDtypeStruct(
+                tuple(c + 2 for c in cells) + (slot_count, 2 * channels), bf16
+            ),
+        ),
+        in_specs=[vmem] * 2,
+        out_specs=(vmem, vmem),
+        scratch_shapes=[dma((devices,)), dma((devices,)), dma((27,)), dma((27,)), dma((2,))],
+        name="gather_atoms",
+        compiler_params=pltpu.CompilerParams(has_side_effects=True),
+    )(atoms, rows)
     ext = ext.astype(f32).reshape(
         (cells_x + 2) * (cells_y + 2), (cells_z + 2) * slot_count, 2 * channels
     )
@@ -458,21 +580,19 @@
     table_k = table_k.reshape(devices, planes)
     phase_c = phase_c.reshape(devices, planes).astype(np.float64)
     taps = [2 * np.pi * ((table_k * t) % length_z) / length_z for t in range(1, 4)]
-    zrow = np.stack(
-        [table_k, phase_c, 1.0 - phase_c]
-        + [np.cos(a) for a in taps]
-        + [np.sin(a) for a in taps],
-        axis=2,
-    ).astype(np.float32)
     basis_x, modes_x = trig_basis(length_x)
     basis_y, modes_y = trig_basis(length_y)
     qx, sx = axis_terms(modes_x, length_x)
     qy, sy = axis_terms(modes_y, length_y)
     qz, sz = axis_terms(table_k, length_z)
-    krow = np.stack(
-        [qz[:, :, None] + qy[None, None, :], sz[:, :, None] * sy[None, None, :]], axis=-1
-    )
-    krow = krow.reshape(devices, planes * length_y, 2).astype(np.float32)
+    krow = np.stack([qy, sy], axis=1).astype(np.float32)
+    zrow = np.stack(
+        [table_k, phase_c, 1.0 - phase_c]
+        + [np.cos(a) for a in taps]
+        + [np.sin(a) for a in taps]
+        + [qz, sz],
+        axis=2,
+    ).astype(np.float32)
     kx = np.stack([qx, sx]).astype(np.float32)
     grid_y = cells_y * CELL
     columns = np.concatenate(
@@ -480,10 +600,9 @@
     )
     by = basis_y[:, columns].astype(np.float32)
     bx = basis_x.astype(np.float32)
-    me = lax.axis_index(AXES)
     partial = pl.pallas_call(
         functools.partial(charge_kernel, sizes, lengths, window, screen, planes),
-        out_shape=jax.ShapeDtypeStruct((sizes[0] * sizes[1], 1, sizes[2] * atom_count), f32),
+        out_shape=jax.ShapeDtypeStruct((devices, 1, atom_count), f32),
         in_specs=[vmem] * 8,
         out_specs=vmem,
         scratch_shapes=[
@@ -496,17 +615,27 @@
         ),
     )(
         atoms,
-        lax.dynamic_index_in_dim(jnp.asarray(zrow), me, 0, False),
-        lax.dynamic_index_in_dim(jnp.asarray(krow), me, 0, False),
+        jnp.asarray(zrow),
+        jnp.asarray(krow),
         jnp.asarray(kx),
         jnp.asarray(by),
         jnp.asarray(np.ascontiguousarray(by.T)),
         jnp.asarray(bx),
         jnp.asarray(np.ascontiguousarray(bx.T)),
     )
-    site_potential = lax.psum_scatter(
-        partial.reshape(devices, atom_count), AXES, scatter_dimension=0, tiled=False
-    )
+    site_potential = pl.pallas_call(
+        functools.partial(scatter_kernel, sizes),
+        out_shape=jax.ShapeDtypeStruct((1, atom_count), f32),
+        in_specs=[vmem],
+        out_specs=vmem,
+        scratch_shapes=[
+            pltpu.VMEM((devices, 1, atom_count), f32),
+            dma((devices,)),
+            dma((devices,)),
+        ],
+        name="scatter_sum",
+        compiler_params=pltpu.CompilerParams(has_side_effects=True),
+    )(partial)
     return (
         updated.reshape(features.shape),
         site_potential.reshape(cells_x, cells_y, cells_z, slot_count),

time: 203 us -> 114 us (0.56)
  blocking collectives: 112 us -> 0 us
  Pallas kernels: 63.3 us -> 98.6 us
  starting transfers between devices: 8.8 us -> 0 us
  local copies, waits for them, and re-layouts: 7.55 us -> 5 us
  waiting for transfers between devices: 2.16 us -> 0 us
    all_gather x1 -> x0, blocking collectives: 74.5 us -> none  [shards(): atoms = lax.all_gather(atoms, AXES)]
    unnamed x1 -> x0, blocking collectives: 37.3 us -> none
    pallas_call x0 -> x2, Pallas kernels: none -> 35.5 us  [the longest x1 22.7 us: shards(): pl.pallas_call(functools.partial(gather_kernel, sizes, cells), out_shape=...]
    ppermute x6 -> x0, starting transfers between devices: 8.8 us -> none  [the longest x3 5.62 us: padded(): high = lax.ppermute(lax.slice_in_dim(block, 0, 1, axis=dim), axis, backward)]
    squeeze x2 -> x0, local copies, waits for them, and re-layouts: 2.94 us -> none  [the longest x1 1.66 us: shards(): lax.dynamic_index_in_dim(jnp.asarray(krow), me, 0, False)]
    reshape x0 -> x1, other arithmetic: none -> 2.56 us  [shards(): ext.astype(f32)]
    ppermute x6 -> x0, waiting for transfers between devices: 2.16 us -> none  [the longest x3 2.16 us: padded(): lax.ppermute(lax.slice_in_dim(block, block.shape[dim] - 1, None, axis=dim...]
  transfers between devices with their start and end apart: 6 -> 0, of which waited for: 1 -> 0; matrix products, arithmetic and copies ran while one was open for 5% -> 0% of each run, Pallas kernels for 8% -> 0%
where the time goes in v1:
time: 114 us; the launch traced here: 113 us
  Pallas kernels  98.6 us (86%)
  other arithmetic  5.78 us (5%)
  local copies, waits for them, and re-layouts  5 us (4%)
  matrix products  3 us (3%)
    pallas_call x1, Pallas kernels, shards(): pl.pallas_call(functools.partial(pair_kernel, (cells_x, cells_y, cells_z)...  47.3 us
    pallas_call x1, Pallas kernels, shards(): pl.pallas_call(functools.partial(gather_kernel, sizes, cells), out_shape=...  22.7 us
    pallas_call x1, Pallas kernels, shards(): pl.pallas_call(functools.partial(charge_kernel, sizes, lengths, window, s...  15.8 us
    pallas_call x1, Pallas kernels, shards(): pl.pallas_call(functools.partial(scatter_kernel, sizes), out_shape=jax.Sh...  12.7 us
    reshape x1, other arithmetic, shards(): ext.astype(f32)  2.56 us

profile of v1, /device:TPU:0, one launch (start us, length us, event | category | flops | bytes accessed | tf_op | source)
XLA Modules:
  0.0 113.2 jit_solution(1907396370514766966)
XLA Ops:
  0.6 0.8 copy.33
  1.5 0.1 reshape.89
  1.7 0.1 reshape.92
  1.8 1.1 convolution_convert_fusion
  3.0 0.1 concatenate.10
  3.1 0.8 copy.36
  4.0 1.0 convolution_reduce_fusion
  5.0 0.8 eq.22
  5.8 0.7 fusion.25
  6.7 0.1 reshape.90
  6.8 0.6 pad_maximum_fusion.atoms_ref
  7.4 22.7 %gather_atoms.1 = (f32[32,4,384]{2,1,0:T(4,128)}, bf16[5,4,10,8,256]{4,3,2,1,0:T(8,128)(2,1)}) custom-call(f32[4,384]{1,0:T(4,128)} %pad_maximum_fusion.atoms_ref, bf16[3,2,8,8,256]{4,3,2,1,0:T(8,128)(2,1)} %bitcast.30), custom_call_target="tpu_custom_call" | custom-call | tf_op jit(solution)/shard_map/gather_atoms/pallas_call | solution.py:507
  30.2 2.6 %convert.21.ext_ref = f32[20,80,256]{2,1,0:T(8,128)} convert(bf16[20,80,256]{2,1,0:T(8,128)(2,1)} %bitcast.29) | non-fusion elementwise | flops 409600 | bytes 2457600 | tf_op jit(solution)/shard_map/reshape | solution.py:521
  32.8 0.4 fusion.10
  33.2 0.1 reshape.88
  33.4 0.2 ge.33
  33.7 0.8 fusion.20.code_ref
  34.4 0.8 fusion.27.own_ref
  35.3 0.7 copy.37.rates_ref
  36.0 47.3 %pair_layer.1 = bf16[384,128]{1,0:T(8,128)(2,1)} custom-call(s32[48,1,512]{2,1,0:T(1,128)} %fusion.20.code_ref, f32[20,80,256]{2,1,0:T(8,128)} %convert.21.ext_ref, f32[384,128]{1,0:T(8,128)} %fusion.27.own_ref, bf16[384,128]{1,0:T(8,128)(2,1)} %bitcast.27, bf16[8,128]{1,0:T(8,128)(2,1)} %wr_ref.1, f32[8,1]{1,0:T(8,128)} %copy.37.rates_ref, ...), custom_call_target="tpu_custom_call" | custom-call | flops 3221225472 | bytes 4194304 | tf_op jit(solution)/shard_map/pair_layer/pallas_call | solution.py:542
  83.3 15.8 %charge_solve.1.part_ref = f32[32,1,384]{2,1,0:T(1,128)} custom-call(f32[32,4,384]{2,1,0:T(4,128)} %get-tuple-element.5.atoms_ref, f32[32,8,11]{2,1,0:T(8,128)} %constant.129.clone.zrow_ref, f32[64,2]{1,0:T(8,128)} %constant.130.clone.krow_ref, f32[2,48]{1,0:T(2,128)} %constant.131.clone.kx_ref, f32[64,96]{1,0:T(8,128)} %constant.132.clone.by_ref, ...), custom_call_target="tpu_custom_call" | custom-call | flops 10000000000 | bytes 2097152 | tf_op jit(solution)/shard_map/charge_solve/pallas_call | solution.py:603
  99.1 12.7 %scatter_sum.1 = f32[1,384]{1,0:T(1,128)} custom-call(f32[32,1,384]{2,1,0:T(1,128)} %charge_solve.1.part_ref), custom_call_target="tpu_custom_call" | custom-call | tf_op jit(solution)/shard_map/scatter_sum/pallas_call | solution.py:626
  111.8 0.7 reduce.1
  112.5 0.7 reshape.98
  (22 shorter events, 0.4 us)
Async XLA Ops:
  0.6 1.2 %copy-start = (bf16[128,128]{1,0:T(8,128)(2,1)S(1)}, bf16[128,128]{1,0:T(8,128)(2,1)}, u32[]{:S(2)}) copy-start(bf16[128,128]{1,0:T(8,128)(2,1)} %param.29) | copy-start | bytes 98308
  3.1 29.6 %copy-start.2 = (s32[3,2,8,512]{3,2,1,0:T(8,128)S(1)}, s32[3,2,8,512]{3,2,1,0:T(8,128)}, u32[]{:S(2)}) copy-start(s32[3,2,8,512]{3,2,1,0:T(8,128)} %param.26) | copy-start | bytes 294916
  6.6 26.7 %copy-start.4 = (s32[3,2,8,8]{3,2,1,0:T(8,128)S(1)}, s32[3,2,8,8]{3,2,1,0:T(8,128)}, u32[]{:S(2)}) copy-start(s32[3,2,8,8]{3,2,1,0:T(8,128)} %param.27) | copy-start | bytes 4612
  30.2 4.3 %copy-start.1 = (bf16[3,2,8,8,128]{4,3,2,1,0:T(8,128)(2,1)S(1)}, bf16[3,2,8,8,128]{4,3,2,1,0:T(8,128)(2,1)}, u32[]{:S(2)}) copy-start(bf16[3,2,8,8,128]{4,3,2,1,0:T(8,128)(2,1)} %param.23) | copy-start | bytes 294916
  30.2 4.3 %copy-start.3 = (bf16[128,128]{1,0:T(8,128)(2,1)S(1)}, bf16[128,128]{1,0:T(8,128)(2,1)}, u32[]{:S(2)}) copy-start(bf16[128,128]{1,0:T(8,128)(2,1)} %param.28) | copy-start | bytes 98308
  30.2 5.1 %copy-start.5 = (f32[8]{0:T(128)S(1)}, f32[8]{0:T(128)}, u32[]{:S(2)}) copy-start(f32[8]{0:T(128)} %param.31) | copy-start | bytes 100

commit v2 on v1

--- a/solution.py
+++ b/solution.py
@@ -152,7 +152,7 @@
             )
         return carry
 
-    lax.fori_loop(0, cells_x * cells_y * cells_z, one_cell, 0)
+    lax.fori_loop(0, cells_x * cells_y * cells_z, one_cell, 0, unroll=8)
     wv = wv_ref[...].astype(f32)
     invariant = None
     for d in range(3):
@@ -286,7 +286,7 @@
             plane_ref[j, rows, :] += total[j * window : (j + 1) * window]
         return carry
 
-    lax.fori_loop(0, devices_x * devices_y, spread_group, 0)
+    lax.fori_loop(0, devices_x * devices_y, spread_group, 0, unroll=2)
 
     def hdot(a, b):
         return jnp.dot(a, b, precision=highest, preferred_element_type=f32)
@@ -329,7 +329,7 @@
             out_ref[g * devices_z + i] = line[:, i * count : (i + 1) * count]
         return carry
 
-    lax.fori_loop(0, devices_x * devices_y, sample_group, 0)
+    lax.fori_loop(0, devices_x * devices_y, sample_group, 0, unroll=2)
 
 
 def coords_of(index, sizes):

time: 114 us -> 98.3 us (0.86)
  Pallas kernels: 98.6 us -> 83.2 us
    pallas_call x1, Pallas kernels: 47.3 us -> 33.5 us  [shards(): pl.pallas_call(functools.partial(pair_kernel, (cells_x, cells_y, cells_z)...]
    pallas_call x1, Pallas kernels: 15.8 us -> 14.3 us  [shards(): pl.pallas_call(functools.partial(charge_kernel, sizes, lengths, window, s...]
where the time goes in v2:
time: 98.3 us; the launch traced here: 97.8 us
  Pallas kernels  83.2 us (85%)
  other arithmetic  5.78 us (6%)
  local copies, waits for them, and re-layouts  5 us (5%)
  matrix products  3 us (3%)
    pallas_call x1, Pallas kernels, shards(): pl.pallas_call(functools.partial(pair_kernel, (cells_x, cells_y, cells_z)...  33.5 us
    pallas_call x1, Pallas kernels, shards(): pl.pallas_call(functools.partial(gather_kernel, sizes, cells), out_shape=...  22.7 us
    pallas_call x1, Pallas kernels, shards(): pl.pallas_call(functools.partial(charge_kernel, sizes, lengths, window, s...  14.3 us
    pallas_call x1, Pallas kernels, shards(): pl.pallas_call(functools.partial(scatter_kernel, sizes), out_shape=jax.Sh...  12.7 us
    reshape x1, other arithmetic, shards(): ext.astype(f32)  2.56 us

profile of v2, /device:TPU:0, one launch (start us, length us, event | category | flops | bytes accessed | tf_op | source)
XLA Modules:
  0.0 97.8 jit_solution(15021884596517508373)
XLA Ops:
  0.6 0.8 copy.33
  1.5 0.1 reshape.89
  1.7 0.1 reshape.92
  1.8 1.1 %convolution_convert_fusion = bf16[384,128]{0,1:T(8,128)(2,1)S(1)} fusion(bf16[384,128]{1,0:T(8,128)(2,1)} %bitcast.25, bf16[128,128]{1,0:T(8,128)(2,1)S(1)} %copy-done), kind=kOutput, calls=%fused_computation | convolution fusion | flops 12632064 | bytes 229376 | tf_op jit(solution)/shard_map/dot_general | solution.py:486
  3.0 0.1 concatenate.10
  3.1 0.8 copy.36
  4.0 1.0 %convolution_reduce_fusion = f32[384]{0:T(512)S(1)} fusion(bf16[384,128]{1,0:T(8,128)(2,1)} %bitcast.26, bf16[128]{0:T(256)(128)(2,1)} %param.36), kind=kOutput, calls=%fused_computation.1 | convolution fusion | flops 98304 | bytes 100096 | tf_op jit(solution)/shard_map/dot_general | solution.py:492
  5.0 0.8 eq.22
  5.8 0.7 fusion.25
  6.7 0.1 reshape.90
  6.8 0.6 pad_maximum_fusion.atoms_ref
  7.4 22.7 %gather_atoms.1 = (f32[32,4,384]{2,1,0:T(4,128)}, bf16[5,4,10,8,256]{4,3,2,1,0:T(8,128)(2,1)}) custom-call(f32[4,384]{1,0:T(4,128)} %pad_maximum_fusion.atoms_ref, bf16[3,2,8,8,256]{4,3,2,1,0:T(8,128)(2,1)} %bitcast.30), custom_call_target="tpu_custom_call" | custom-call | tf_op jit(solution)/shard_map/gather_atoms/pallas_call | solution.py:507
  30.2 2.6 %convert.21.ext_ref = f32[20,80,256]{2,1,0:T(8,128)} convert(bf16[20,80,256]{2,1,0:T(8,128)(2,1)} %bitcast.29) | non-fusion elementwise | flops 409600 | bytes 2457600 | tf_op jit(solution)/shard_map/reshape | solution.py:521
  32.8 0.4 fusion.10
  33.2 0.1 reshape.88
  33.4 0.2 ge.33
  33.7 0.8 fusion.20.code_ref
  34.4 0.8 fusion.27.own_ref
  35.3 0.7 copy.37.rates_ref
  36.0 33.5 %pair_layer.1 = bf16[384,128]{1,0:T(8,128)(2,1)} custom-call(s32[48,1,512]{2,1,0:T(1,128)} %fusion.20.code_ref, f32[20,80,256]{2,1,0:T(8,128)} %convert.21.ext_ref, f32[384,128]{1,0:T(8,128)} %fusion.27.own_ref, bf16[384,128]{1,0:T(8,128)(2,1)} %bitcast.27, bf16[8,128]{1,0:T(8,128)(2,1)} %wr_ref.1, f32[8,1]{1,0:T(8,128)} %copy.37.rates_ref, ...), custom_call_target="tpu_custom_call" | custom-call | flops 3221225472 | bytes 4194304 | tf_op jit(solution)/shard_map/pair_layer/pallas_call | solution.py:542
  69.4 14.3 %charge_solve.1.part_ref = f32[32,1,384]{2,1,0:T(1,128)} custom-call(f32[32,4,384]{2,1,0:T(4,128)} %get-tuple-element.5.atoms_ref, f32[32,8,11]{2,1,0:T(8,128)} %constant.129.clone.zrow_ref, f32[64,2]{1,0:T(8,128)} %constant.130.clone.krow_ref, f32[2,48]{1,0:T(2,128)} %constant.131.clone.kx_ref, f32[64,96]{1,0:T(8,128)} %constant.132.clone.by_ref, ...), custom_call_target="tpu_custom_call" | custom-call | flops 10000000000 | bytes 2097152 | tf_op jit(solution)/shard_map/charge_solve/pallas_call | solution.py:603
  83.7 12.7 %scatter_sum.1 = f32[1,384]{1,0:T(1,128)} custom-call(f32[32,1,384]{2,1,0:T(1,128)} %charge_solve.1.part_ref), custom_call_target="tpu_custom_call" | custom-call | tf_op jit(solution)/shard_map/scatter_sum/pallas_call | solution.py:626
  96.4 0.7 reduce.1
  97.1 0.7 reshape.98
  (22 shorter events, 0.4 us)
Async XLA Ops:
  0.6 1.2 %copy-start = (bf16[128,128]{1,0:T(8,128)(2,1)S(1)}, bf16[128,128]{1,0:T(8,128)(2,1)}, u32[]{:S(2)}) copy-start(bf16[128,128]{1,0:T(8,128)(2,1)} %param.29) | copy-start | bytes 98308
  3.1 29.6 %copy-start.2 = (s32[3,2,8,512]{3,2,1,0:T(8,128)S(1)}, s32[3,2,8,512]{3,2,1,0:T(8,128)}, u32[]{:S(2)}) copy-start(s32[3,2,8,512]{3,2,1,0:T(8,128)} %param.26) | copy-start | bytes 294916
  6.6 26.7 %copy-start.4 = (s32[3,2,8,8]{3,2,1,0:T(8,128)S(1)}, s32[3,2,8,8]{3,2,1,0:T(8,128)}, u32[]{:S(2)}) copy-start(s32[3,2,8,8]{3,2,1,0:T(8,128)} %param.27) | copy-start | bytes 4612
  30.2 4.3 %copy-start.1 = (bf16[3,2,8,8,128]{4,3,2,1,0:T(8,128)(2,1)S(1)}, bf16[3,2,8,8,128]{4,3,2,1,0:T(8,128)(2,1)}, u32[]{:S(2)}) copy-start(bf16[3,2,8,8,128]{4,3,2,1,0:T(8,128)(2,1)} %param.23) | copy-start | bytes 294916
  30.2 4.3 %copy-start.3 = (bf16[128,128]{1,0:T(8,128)(2,1)S(1)}, bf16[128,128]{1,0:T(8,128)(2,1)}, u32[]{:S(2)}) copy-start(bf16[128,128]{1,0:T(8,128)(2,1)} %param.28) | copy-start | bytes 98308
  30.2 5.1 %copy-start.5 = (f32[8]{0:T(128)S(1)}, f32[8]{0:T(128)}, u32[]{:S(2)}) copy-start(f32[8]{0:T(128)} %param.31) | copy-start | bytes 100
